TPU v7x, 32 devices: a whole 2x2x4 slice. The times are simulated.
32 devices in a mesh: fsdp: 8 (over z, y), rep: 4 (over x, core).
Axes of the slice: x: 2, y: 2, z: 4, core: 2. Of those that a mesh axis runs over, the one named last changes fastest.
Arguments:
- partial_grad: bfloat16 [4, 8, 1024, 1024], P('rep', None, 'fsdp'), may hold values from -3 to 3
- owner_table: int32 [8, 2], replicated, may hold values from -1 to 7, as said below
- left_stat: float32 [8, 2, 1024, 1024], P('fsdp', None, None, 'rep'), may hold values from -6 to 6
- right_stat: float32 [8, 2, 1024, 1024], P('fsdp', None, None, 'rep'), may hold values from -6 to 6
- left_root: bfloat16 [8, 2, 1024, 1024], P('fsdp', None, None, 'rep'), may hold values from -0.1875 to 0.1875
- right_root: bfloat16 [8, 2, 1024, 1024], P('fsdp', None, None, 'rep'), may hold values from -0.1875 to 0.1875
Outputs:
- left_new: float32 [8, 2, 1024, 1024], P('fsdp', None, None, 'rep')
- right_new: float32 [8, 2, 1024, 1024], P('fsdp', None, None, 'rep')
- update: bfloat16 [8, 1024, 1024], P(None, 'fsdp', 'rep')
Inputs may be any that keep to these rules, and one draw needn't show every extreme that they name: `owner_table`: each of the 8 blocks stands in exactly one slot and -1 marks an empty slot; some owner fills all 2 slots and some owner has none.
All inputs are finite; a program needn't handle non-finite values.
Results may differ from a plain program's by a relative error of at most 0.014.
Values may be sent and summed in bfloat16 or wider, within the bound.
No kernel may reach another device: no remote copies, remote signals or barrier semaphores. Data moves between devices by JAX's collectives and lax.ppermute only.
A program may use at most 64 MiB of HBM per device.

v0:
```python
import jax
import jax.numpy as jnp
from jax import lax
from jax.sharding import PartitionSpec as P

decay_rate = 0.99


def on_device(partial_grad, owner_table, left_stat, right_stat, left_root, right_root):
    local_grad = partial_grad[0]
    block_count = local_grad.shape[0]
    my_row = lax.dynamic_index_in_dim(owner_table, lax.axis_index("fsdp"), 0, keepdims=False)
    is_filled = my_row >= 0
    sender_index = jnp.maximum(owner_table.T, 0)
    sender_mask = owner_table.T >= 0
    shares = lax.psum_scatter(
        local_grad.astype(jnp.float32).astype(jnp.bfloat16), "rep", scatter_dimension=2, tiled=True
    )
    picked = jnp.take(shares, sender_index, axis=0)
    picked = jnp.where(sender_mask[:, :, None, None], picked, jnp.zeros((), picked.dtype))
    columns = lax.all_to_all(
        picked.reshape(picked.shape[0], -1, picked.shape[3]),
        "fsdp",
        split_axis=1,
        concat_axis=1,
        tiled=True,
    )
    gradient = lax.all_gather(columns, "rep", axis=2, tiled=True)
    share_width = left_stat.shape[3]
    first_col = lax.axis_index("rep") * share_width
    rows_share = lax.dynamic_slice_in_dim(gradient, first_col, share_width, 1)
    cols_share = lax.dynamic_slice_in_dim(gradient, first_col, share_width, 2)
    left_term = jnp.einsum("sik,sjk->sij", gradient, rows_share, preferred_element_type=jnp.float32)
    right_term = jnp.einsum(
        "ski,skj->sij", gradient, cols_share, preferred_element_type=jnp.float32
    )
    keeper = is_filled[:, None, None]
    left_next = jnp.where(
        keeper, decay_rate * left_stat[0] + (1.0 - decay_rate) * left_term, left_stat[0]
    )
    right_next = jnp.where(
        keeper, decay_rate * right_stat[0] + (1.0 - decay_rate) * right_term, right_stat[0]
    )
    applied = jnp.einsum(
        "sik,skj->sij",
        lax.all_gather(left_root[0], "rep", axis=2, tiled=True),
        gradient,
        preferred_element_type=jnp.float32,
    ).astype(jnp.bfloat16)
    result_cols = jnp.einsum(
        "sik,skj->sij", applied, right_root[0], preferred_element_type=jnp.float32
    ).astype(jnp.bfloat16)
    returned = lax.all_to_all(result_cols, "fsdp", split_axis=1, concat_axis=0, tiled=True)
    flat_table = owner_table.reshape(-1)
    slot_ids = jnp.arange(flat_table.shape[0], dtype=jnp.int32)
    block_ids = jnp.arange(block_count, dtype=jnp.int32)
    positions = jnp.sum(
        jnp.where(flat_table[None, :] == block_ids[:, None], slot_ids[None, :], 0), axis=1
    )
    update = jnp.take(returned, positions, axis=0)
    return (left_next[None], right_next[None], update)


def solution(mesh):
    return jax.shard_map(
        on_device,
        mesh=mesh,
        in_specs=(
            P("rep", None, "fsdp", None),
            P(),
            P("fsdp", None, None, "rep"),
            P("fsdp", None, None, "rep"),
            P("fsdp", None, None, "rep"),
            P("fsdp", None, None, "rep"),
        ),
        out_specs=(
            P("fsdp", None, None, "rep"),
            P("fsdp", None, None, "rep"),
            P(None, "fsdp", "rep"),
        ),
        check_vma=False,
    )
```

profile of v0, /device:TPU:0, one launch (start us, length us, event | category | flops | bytes accessed | tf_op | source)
XLA Modules:
  0.0 170.1 jit_solution(2735394884367178796)
XLA Ops:
  7.2 0.7 reduce-scatter.2.cloned.1.call-update
  8.0 0.7 all-gather.6.cloned.1.call-update
  8.7 0.1 reshape.44
  9.0 35.4 %reduce-scatter.2.cloned.1.call-done = bf16[8,128,256]{2,1,0:T(8,128)(2,1)} async-done(((bf16[8,128,1024]{2,1,0:T(8,128)(2,1)}), bf16[8,128,256]{2,1,0:T(8,128)(2,1)}) %reduce-scatter.2.cloned.1.call-update) | async-done | bytes 524304 | tf_op jit(solution)/shard_map/reduce_scatter | solution.py:16
  44.4 1.7 gather_fusion
  46.1 0.9 fusion.18
  47.1 1.1 copy.31
  48.1 30.9 %all_to_all.23 = bf16[2,1024,256]{2,0,1:T(2,128)(2,1)S(1)} all-to-all(bf16[2,1024,256]{2,0,1:T(2,128)(2,1)S(1)} %copy.31), channel_id=1, replica_groups=mesh['fsdp'=8,'rep'=4] {'fsdp'}, dimensions={1} | all-to-all | bytes 2097152 | tf_op jit(solution)/shard_map/all_to_all | solution.py:21
  79.1 1.1 copy.32
  80.2 0.8 all-gather.6.cloned.1.call-done
  81.0 37.2 %all-gather.4.cloned.1.call-done = bf16[2,1024,1024]{2,1,0:T(8,128)(2,1)} async-done(((bf16[2,1024,256]{2,1,0:T(8,128)(2,1)}), bf16[2,1024,1024]{2,1,0:T(8,128)(2,1)}) %all-gather.4.cloned.1.call-update) | async-done | bytes 4194320 | tf_op jit(solution)/shard_map/all_gather | solution.py:28
  118.2 9.9 %fusion.12 = bf16[2,1024,256]{2,1,0:T(8,128)(2,1)S(1)} fusion(bf16[2,1024,1024]{2,1,0:T(8,128)(2,1)} %all-gather.4.cloned.1.call-done, bf16[1,2,1024,1024]{3,2,1,0:T(8,128)(2,1)} %all-gather.6.cloned.1.call-done, bf16[1,2,1024,256]{3,2,1,0:T(8,128)(2,1)S(1)} %copy-done), kind=kOutput, calls=%fused_computation.14 | convolution fusion | flops 5371330560 | bytes 10485760 | tf_op jit(solution)/shard_map/sik,skj->sij/dot_general | solution.py:50
  128.1 2.0 %copy.37 = bf16[2,1024,256]{2,0,1:T(2,128)(2,1)} copy(bf16[2,1024,256]{2,1,0:T(8,128)(2,1)S(1)} %fusion.12) | data formatting | bytes 2097152 | tf_op jit(solution)/shard_map/convert_element_type | solution.py:52
  130.1 5.5 %all-to-all-start.1 = ((bf16[2,1024,256]{2,0,1:T(2,128)(2,1)}), bf16[2,1024,256]{2,0,1:T(2,128)(2,1)S(1)}, u32[]{:S(2)}, u32[]{:S(2)}) async-start(bf16[2,1024,256]{2,0,1:T(2,128)(2,1)} %copy.37), calls=%async_computation.2 | async-start | bytes 2097152 | tf_op jit(solution)/shard_map/all_to_all | solution.py:53
  135.7 0.1 eq.15
  135.8 0.2 compare_reduce_fusion
  136.0 0.1 select_reduce_fusion
  136.2 6.4 %fusion.5 = f32[1,2,1024,256]{3,2,1,0:T(8,128)} fusion(f32[1,2,1024,256]{3,2,1,0:T(8,128)} %param.9, bf16[2,1024,1024]{2,1,0:T(8,128)(2,1)} %all-gather.4.cloned.1.call-done, s32[]{:T(128)S(6)} %select_n.55, pred[2]{0:T(512)(128)(4,1)S(1)} %compare_reduce_fusion), kind=kOutput, calls=%fused_computation.9 | convolution fusion | flops 1075838976 | bytes 9437190 | tf_op jit(solution)/shard_map/ski,skj->sij/dot_general | solution.py:34
  142.6 2.7 %fusion.7 = f32[1,2,1024,256]{3,2,1,0:T(8,128)} fusion(f32[1,2,1024,256]{3,2,1,0:T(8,128)S(1)} %copy-done.3, bf16[2,1024,1024]{2,1,0:T(8,128)(2,1)S(1)} %copy-done.2, s32[]{:T(128)S(6)} %select_n.55, pred[2]{0:T(512)(128)(4,1)S(1)} %compare_reduce_fusion), kind=kOutput, calls=%fused_computation.13 | convolution fusion | flops 1075838976 | bytes 9437700 | tf_op jit(solution)/shard_map/sik,sjk->sij/dot_general | solution.py:33
  145.4 16.5 %all-to-all-done.1 = bf16[2,1024,256]{2,0,1:T(2,128)(2,1)S(1)} async-done(((bf16[2,1024,256]{2,0,1:T(2,128)(2,1)}), bf16[2,1024,256]{2,0,1:T(2,128)(2,1)S(1)}, u32[]{:S(2)}, u32[]{:S(2)}) %all-to-all-start.1) | async-done | bytes 1048608 | tf_op jit(solution)/shard_map/all_to_all | solution.py:53
  161.8 0.1 copy.38
  162.0 0.1 copy.39
  162.1 0.6 gather_fusion.1
  162.7 0.9 broadcast_select_fusion
  (23 shorter events, 0.4 us)
Async XLA Ops:
  7.2 111.1 %copy-start = (bf16[1,2,1024,256]{3,2,1,0:T(8,128)(2,1)S(1)}, bf16[1,2,1024,256]{3,2,1,0:T(8,128)(2,1)}, u32[]{:S(2)}) copy-start(bf16[1,2,1024,256]{3,2,1,0:T(8,128)(2,1)} %param.11) | copy-start | bytes 3145732
  7.2 1.5 copy-start.1
  7.2 37.3 %reduce-scatter.2.cloned.1.call-start = ((), (), s32[]{:S(2)}) async-start(), calls=%async_computation.3 | async-start | bytes 2621440 | tf_op jit(solution)/shard_map/reduce_scatter | solution.py:16
  7.9 73.1 %all-gather.6.cloned.1.call-start = ((), (), s32[]{:S(2)}) async-start(), calls=%async_computation.5 | async-start | bytes 5242880 | tf_op jit(solution)/shard_map/all_gather | solution.py:46
  8.7 109.5 %all-gather.4.cloned.1.call-start = ((), (), s32[]{:S(2)}) async-start(), calls=%async_computation.4 | async-start | bytes 5242880 | tf_op jit(solution)/shard_map/all_gather | solution.py:28
  130.1 31.7 %all-to-all-start.1 = ((bf16[2,1024,256]{2,0,1:T(2,128)(2,1)}), bf16[2,1024,256]{2,0,1:T(2,128)(2,1)S(1)}, u32[]{:S(2)}, u32[]{:S(2)}) async-start(bf16[2,1024,256]{2,0,1:T(2,128)(2,1)} %copy.37), calls=%async_computation.2 | async-start | bytes 2097152 | tf_op jit(solution)/shard_map/all_to_all | solution.py:53
  136.1 6.5 %copy-start.2 = (bf16[2,1024,1024]{2,1,0:T(8,128)(2,1)S(1)}, bf16[2,1024,1024]{2,1,0:T(8,128)(2,1)}, u32[]{:S(2)}) copy-start(bf16[2,1024,1024]{2,1,0:T(8,128)(2,1)} %all-gather.4.cloned.1.call-done) | copy-start | bytes 12582916
  136.2 6.5 %copy-start.3 = (f32[1,2,1024,256]{3,2,1,0:T(8,128)S(1)}, f32[1,2,1024,256]{3,2,1,0:T(8,128)}, u32[]{:S(2)}) copy-start(f32[1,2,1024,256]{3,2,1,0:T(8,128)} %param.8) | copy-start | bytes 6291460
Sparse Core Ops, SparseCore 0:
  10.5 33.8 reduce-scatter.1
  46.0 34.9 all-gather.5
  83.2 34.9 all-gather.3
where the time goes:
time: 170 us
  waiting for transfers between devices  91.3 us (54%)
  blocking collectives  30.9 us (18%)
  matrix products  19 us (11%)
  between operations  13.9 us (8%)
  local copies, waits for them, and re-layouts  7.14 us (4%)
  starting transfers between devices  5.63 us (3%)
  other arithmetic  2.2 us (1%)
    all_gather x1, waiting for transfers between devices, on_device(): gradient = lax.all_gather(columns, 'rep', axis=2, tiled=True)  37.2 us
    reduce_scatter x1, waiting for transfers between devices, on_device(): lax.psum_scatter(local_grad.astype(jnp.float32).astype(jnp.bfloat16), 're...  35.4 us
    all_to_all x1, blocking collectives, on_device(): lax.all_to_all(picked.reshape(picked.shape[0], -1, picked.shape[3]), 'fsd...  30.9 us
    all_to_all x1, waiting for transfers between devices, on_device(): lax.all_to_all(result_cols, 'fsdp', split_axis=1, concat_axis=0, tiled=True)  16.5 us
    dot_general x1, matrix products, on_device(): jnp.einsum('sik,skj->sij', applied, right_root[0], preferred_element_type...  9.85 us
    dot_general x1, matrix products, on_device(): jnp.einsum('ski,skj->sij', gradient, cols_share, preferred_element_type=j...  6.45 us
    all_to_all x1, starting transfers between devices, on_device(): lax.all_to_all(result_cols, 'fsdp', split_axis=1, concat_axis=0, tiled=True)  5.52 us
  transfers between devices with their start and end apart: 4, of which 4 were waited for; matrix products, arithmetic and copies ran while one was open for 9% of the time, Pallas kernels for 0%

commit v1 on v0

--- a/solution.py
+++ b/solution.py
@@ -18,12 +18,15 @@
     )
     picked = jnp.take(shares, sender_index, axis=0)
     picked = jnp.where(sender_mask[:, :, None, None], picked, jnp.zeros((), picked.dtype))
-    columns = lax.all_to_all(
-        picked.reshape(picked.shape[0], -1, picked.shape[3]),
-        "fsdp",
-        split_axis=1,
-        concat_axis=1,
-        tiled=True,
+    work_x = picked.reshape(picked.shape[0], -1, picked.shape[3])
+    columns = jnp.concatenate(
+        lax.all_to_all(
+            jnp.stack(jnp.split(work_x, lax.axis_size("fsdp"), axis=1)),
+            axis_name="fsdp",
+            split_axis=0,
+            concat_axis=0,
+        ),
+        axis=1,
     )
     gradient = lax.all_gather(columns, "rep", axis=2, tiled=True)
     share_width = left_stat.shape[3]

time: 170 us -> 170 us (level)
  transfers between devices with their start and end apart: 4 -> 4, of which waited for: 4 -> 4; matrix products, arithmetic and copies ran while one was open for 9% -> 8% of each run, Pallas kernels for 0% -> 0%
where the time goes in v1:
time: 170 us
  waiting for transfers between devices  92.3 us (54%)
  blocking collectives  30.9 us (18%)
  matrix products  19 us (11%)
  between operations  13.9 us (8%)
  local copies, waits for them, and re-layouts  6.08 us (4%)
  starting transfers between devices  5.63 us (3%)
  other arithmetic  2.2 us (1%)
    all_gather x1, waiting for transfers between devices, on_device(): gradient = lax.all_gather(columns, 'rep', axis=2, tiled=True)  37.2 us
    reduce_scatter x1, waiting for transfers between devices, on_device(): lax.psum_scatter(local_grad.astype(jnp.float32).astype(jnp.bfloat16), 're...  35.4 us
    all_to_all x1, blocking collectives, on_device(): lax.all_to_all(jnp.stack(jnp.split(work_x, lax.axis_size('fsdp'), axis=1)...  30.9 us
    all_to_all x1, waiting for transfers between devices, on_device(): lax.all_to_all(result_cols, 'fsdp', split_axis=1, concat_axis=0, tiled=True)  16.5 us
    dot_general x1, matrix products, on_device(): jnp.einsum('sik,skj->sij', applied, right_root[0], preferred_element_type...  9.85 us
    dot_general x1, matrix products, on_device(): jnp.einsum('ski,skj->sij', gradient, cols_share, preferred_element_type=j...  6.45 us
    all_to_all x1, starting transfers between devices, on_device(): lax.all_to_all(result_cols, 'fsdp', split_axis=1, concat_axis=0, tiled=True)  5.52 us
  transfers between devices with their start and end apart: 4, of which 4 were waited for; matrix products, arithmetic and copies ran while one was open for 8% of the time, Pallas kernels for 0%

profile of v1, /device:TPU:0, one launch (start us, length us, event | category | flops | bytes accessed | tf_op | source)
XLA Modules:
  0.0 170.1 jit_solution(8760038868949579486)
XLA Ops:
  7.2 0.7 reduce-scatter.2.cloned.1.call-update
  8.0 0.7 all-gather.6.cloned.1.call-update
  8.7 0.1 reshape.52
  9.0 35.4 %reduce-scatter.2.cloned.1.call-done = bf16[8,128,256]{2,1,0:T(8,128)(2,1)} async-done(((bf16[8,128,1024]{2,1,0:T(8,128)(2,1)}), bf16[8,128,256]{2,1,0:T(8,128)(2,1)}) %reduce-scatter.2.cloned.1.call-update) | async-done | bytes 524304 | tf_op jit(solution)/shard_map/reduce_scatter | solution.py:16
  44.4 1.7 gather_fusion
  46.1 0.9 fusion.18
  47.2 30.9 %all_to_all.23 = bf16[8,2,128,256]{3,2,1,0:T(8,128)(2,1)S(1)} all-to-all(bf16[8,2,128,256]{3,2,1,0:T(8,128)(2,1)S(1)} %fusion.21), channel_id=1, replica_groups=mesh['fsdp'=8,'rep'=4] {'fsdp'}, dimensions={0} | all-to-all | bytes 2097152 | tf_op jit(solution)/shard_map/all_to_all | solution.py:23
  78.1 1.0 copy.42
  79.2 1.9 %all-gather.6.cloned.1.call-done = bf16[1,2,1024,1024]{3,2,1,0:T(8,128)(2,1)} async-done(((bf16[1,2,1024,256]{3,2,1,0:T(8,128)(2,1)}), bf16[1,2,1024,1024]{3,2,1,0:T(8,128)(2,1)}) %all-gather.6.cloned.1.call-update) | async-done | bytes 4194320 | tf_op jit(solution)/shard_map/all_gather | solution.py:49
  81.0 37.2 %all-gather.4.cloned.1.call-done = bf16[2,1024,1024]{2,1,0:T(8,128)(2,1)} async-done(((bf16[2,1024,256]{2,1,0:T(8,128)(2,1)}), bf16[2,1024,1024]{2,1,0:T(8,128)(2,1)}) %all-gather.4.cloned.1.call-update) | async-done | bytes 4194320 | tf_op jit(solution)/shard_map/all_gather | solution.py:31
  118.2 9.9 %fusion.12 = bf16[2,1024,256]{2,1,0:T(8,128)(2,1)S(1)} fusion(bf16[2,1024,1024]{2,1,0:T(8,128)(2,1)} %all-gather.4.cloned.1.call-done, bf16[1,2,1024,1024]{3,2,1,0:T(8,128)(2,1)} %all-gather.6.cloned.1.call-done, bf16[1,2,1024,256]{3,2,1,0:T(8,128)(2,1)S(1)} %copy-done), kind=kOutput, calls=%fused_computation.14 | convolution fusion | flops 5371330560 | bytes 10485760 | tf_op jit(solution)/shard_map/sik,skj->sij/dot_general | solution.py:53
  128.1 2.0 %copy.47 = bf16[2,1024,256]{2,0,1:T(2,128)(2,1)} copy(bf16[2,1024,256]{2,1,0:T(8,128)(2,1)S(1)} %fusion.12) | data formatting | bytes 2097152 | tf_op jit(solution)/shard_map/convert_element_type | solution.py:55
  130.1 5.5 %all-to-all-start.1 = ((bf16[2,1024,256]{2,0,1:T(2,128)(2,1)}), bf16[2,1024,256]{2,0,1:T(2,128)(2,1)S(1)}, u32[]{:S(2)}, u32[]{:S(2)}) async-start(bf16[2,1024,256]{2,0,1:T(2,128)(2,1)} %copy.47), calls=%async_computation.2 | async-start | bytes 2097152 | tf_op jit(solution)/shard_map/all_to_all | solution.py:56
  135.6 0.1 copy.44
  135.7 0.1 eq.15
  135.8 0.2 compare_reduce_fusion
  136.0 0.1 select_reduce_fusion
  136.2 6.4 %fusion.5 = f32[1,2,1024,256]{3,2,1,0:T(8,128)} fusion(f32[1,2,1024,256]{3,2,1,0:T(8,128)} %param.9, bf16[2,1024,1024]{2,1,0:T(8,128)(2,1)} %all-gather.4.cloned.1.call-done, s32[]{:T(128)S(6)} %select_n.55, pred[2]{0:T(512)(128)(4,1)S(1)} %compare_reduce_fusion), kind=kOutput, calls=%fused_computation.9 | convolution fusion | flops 1075838976 | bytes 9437190 | tf_op jit(solution)/shard_map/ski,skj->sij/dot_general | solution.py:37
  142.6 2.7 %fusion.7 = f32[1,2,1024,256]{3,2,1,0:T(8,128)} fusion(f32[1,2,1024,256]{3,2,1,0:T(8,128)S(1)} %copy-done.3, bf16[2,1024,1024]{2,1,0:T(8,128)(2,1)S(1)} %copy-done.2, s32[]{:T(128)S(6)} %select_n.55, pred[2]{0:T(512)(128)(4,1)S(1)} %compare_reduce_fusion), kind=kOutput, calls=%fused_computation.13 | convolution fusion | flops 1075838976 | bytes 9437700 | tf_op jit(solution)/shard_map/sik,sjk->sij/dot_general | solution.py:36
  145.4 16.5 %all-to-all-done.1 = bf16[2,1024,256]{2,0,1:T(2,128)(2,1)S(1)} async-done(((bf16[2,1024,256]{2,0,1:T(2,128)(2,1)}), bf16[2,1024,256]{2,0,1:T(2,128)(2,1)S(1)}, u32[]{:S(2)}, u32[]{:S(2)}) %all-to-all-start.1) | async-done | bytes 1048608 | tf_op jit(solution)/shard_map/all_to_all | solution.py:56
  161.8 0.1 copy.48
  162.0 0.1 copy.49
  162.1 0.6 gather_fusion.1
  162.7 0.9 broadcast_select_fusion
  (30 shorter events, 0.5 us)
Async XLA Ops:
  7.2 111.0 %copy-start = (bf16[1,2,1024,256]{3,2,1,0:T(8,128)(2,1)S(1)}, bf16[1,2,1024,256]{3,2,1,0:T(8,128)(2,1)}, u32[]{:S(2)}) copy-start(bf16[1,2,1024,256]{3,2,1,0:T(8,128)(2,1)} %param.11) | copy-start | bytes 3145732
  7.2 1.5 copy-start.1
  7.2 37.3 %reduce-scatter.2.cloned.1.call-start = ((), (), s32[]{:S(2)}) async-start(), calls=%async_computation.3 | async-start | bytes 2621440 | tf_op jit(solution)/shard_map/reduce_scatter | solution.py:16
  7.9 73.1 %all-gather.6.cloned.1.call-start = ((), (), s32[]{:S(2)}) async-start(), calls=%async_computation.5 | async-start | bytes 5242880 | tf_op jit(solution)/shard_map/all_gather | solution.py:49
  8.7 109.5 %all-gather.4.cloned.1.call-start = ((), (), s32[]{:S(2)}) async-start(), calls=%async_computation.4 | async-start | bytes 5242880 | tf_op jit(solution)/shard_map/all_gather | solution.py:31
  130.1 31.7 %all-to-all-start.1 = ((bf16[2,1024,256]{2,0,1:T(2,128)(2,1)}), bf16[2,1024,256]{2,0,1:T(2,128)(2,1)S(1)}, u32[]{:S(2)}, u32[]{:S(2)}) async-start(bf16[2,1024,256]{2,0,1:T(2,128)(2,1)} %copy.47), calls=%async_computation.2 | async-start | bytes 2097152 | tf_op jit(solution)/shard_map/all_to_all | solution.py:56
  136.1 6.5 %copy-start.2 = (bf16[2,1024,1024]{2,1,0:T(8,128)(2,1)S(1)}, bf16[2,1024,1024]{2,1,0:T(8,128)(2,1)}, u32[]{:S(2)}) copy-start(bf16[2,1024,1024]{2,1,0:T(8,128)(2,1)} %all-gather.4.cloned.1.call-done) | copy-start | bytes 12582916
  136.1 6.5 %copy-start.3 = (f32[1,2,1024,256]{3,2,1,0:T(8,128)S(1)}, f32[1,2,1024,256]{3,2,1,0:T(8,128)}, u32[]{:S(2)}) copy-start(f32[1,2,1024,256]{3,2,1,0:T(8,128)} %param.8) | copy-start | bytes 6291460
Sparse Core Ops, SparseCore 0:
  10.5 33.8 reduce-scatter.1
  46.0 34.9 all-gather.5
  83.2 34.9 all-gather.3
